TPU v7x, 128 devices: a whole 4x4x4 slice. The times are simulated.
128 devices in a mesh: dp: 8 (over z, core), tp: 16 (over y, x).
Axes of the slice: x: 4, y: 4, z: 4, core: 2. Of those that a mesh axis runs over, the one named last changes fastest.
Arguments:
- head_fsdp: bfloat16 [4096, 128256], P(('dp', 'tp')), may hold values from -0.5 to 0.5
- hidden: bfloat16 [2048, 4096], P(('dp', 'tp')), may hold values from -48 to 48
- targets: int32 [2048], P(('dp', 'tp')), may hold values from 0 to 128255
Outputs:
- head_tp: bfloat16 [4096, 128256], P('dp', 'tp')
- log_norm: float32 [2048], P(('dp', 'tp'))
- target_logprob: float32 [2048], P(('dp', 'tp'))
All inputs are finite; a program needn't handle non-finite values.
Results may differ from a plain program's by a relative error of at most 0.0004.
Values may be sent and summed in bfloat16 or wider, within the bound.
No kernel may reach another device: no remote copies, remote signals or barrier semaphores. Data moves between devices by JAX's collectives and lax.ppermute only.
A program may use at most 192 MiB of HBM per device.

v0:
```python
import jax
import jax.numpy as jnp
from jax import lax
from jax.sharding import Mesh
from jax.sharding import PartitionSpec as P

TP = ("tp_0", "tp_1")
DP = ("dp_0", "dp_1")
DP_TP = ("dp_0", "dp_1", "tp_0", "tp_1")


def all_in_one(shard, axis):
    leaves = jax.tree.leaves(shard)
    order = sorted(range(len(leaves)), key=lambda k: -leaves[k].size)
    width = (1, *leaves[order[0]].shape)[-1]
    lines = [
        jnp.pad(leaves[k].reshape(-1), (0, -leaves[k].size % width)).reshape(-1, width)
        for k in order
    ]
    both, at, found = (lax.all_gather(jnp.concatenate(lines), axis), 0, {})
    for k, line in zip(order, lines):
        piece = both[:, at : at + len(line)].reshape(len(both), -1)
        found[k] = piece[:, : leaves[k].size].reshape(-1, *leaves[k].shape)
        at += len(line)
    numbers = iter(range(len(leaves)))
    return jax.tree.map(lambda _: found[next(numbers)], shard)


def joined_all(shard, axes, combine):
    for axis in axes:
        pieces = all_in_one(shard, axis)
        shard = jax.tree.map(lambda part: part[0], pieces)
        for k in range(1, lax.axis_size(axis)):
            shard = combine(shard, jax.tree.map(lambda part: part[k], pieces))
    return shard


def combine_rows(earlier, later):
    peak_one, mass_one, pick_one = earlier
    peak_two, mass_two, pick_two = later
    highest = jnp.maximum(peak_one, peak_two)
    joined = mass_one * jnp.exp(peak_one - highest) + mass_two * jnp.exp(peak_two - highest)
    return (highest, joined, pick_one + pick_two)


def shards(head_fsdp, hidden, targets):
    head_tp = lax.all_to_all(head_fsdp, TP, split_axis=1, concat_axis=0, tiled=True)
    head_full = lax.all_to_all(head_tp, DP, split_axis=1, concat_axis=0, tiled=True)
    vocab_start = lax.axis_index(TP) * head_tp.shape[1] + lax.axis_index(DP) * head_full.shape[1]
    all_hidden, all_targets = (
        lax.all_gather(hidden, DP_TP, axis=0, tiled=True),
        lax.all_gather(targets, DP_TP, axis=0, tiled=True),
    )
    logits = jnp.dot(all_hidden, head_full, preferred_element_type=jnp.float32)
    local_peak = jnp.max(logits, axis=1)
    offset = all_targets - vocab_start
    columns = lax.broadcasted_iota(jnp.int32, logits.shape, 1)
    picked = jnp.sum(jnp.where(columns == offset[:, None], logits, 0.0), axis=1)
    local_mass = jnp.sum(jnp.exp(logits - local_peak[:, None]), axis=1)
    top_logit, total_mass, target_logit = joined_all(
        (local_peak, local_mass, picked), DP_TP, combine_rows
    )
    log_norm = top_logit + jnp.log(total_mass)
    logprob = target_logit - log_norm
    own_rows = hidden.shape[0]
    row_start = (lax.axis_index(DP) * lax.axis_size(TP) + lax.axis_index(TP)) * own_rows
    own_norm = lax.dynamic_slice_in_dim(log_norm, row_start, own_rows, 0)
    own_logprob = lax.dynamic_slice_in_dim(logprob, row_start, own_rows, 0)
    return (head_tp, own_norm, own_logprob)


def solution(mesh):
    split = Mesh(mesh.devices.reshape(4, 2, 4, 4), ("dp_0", "dp_1", "tp_0", "tp_1"))
    placed = (P(DP_TP, None), P(DP_TP, None), P(DP_TP))
    return jax.shard_map(
        shards,
        mesh=split,
        in_specs=placed,
        out_specs=(P(DP, TP), P(DP_TP), P(DP_TP)),
        check_vma=False,
    )
```

profile of v0, /device:TPU:0, one launch (start us, length us, event | category | flops | bytes accessed | tf_op | source)
XLA Modules:
  0.0 437.6 jit_solution(9103793541087411088)
XLA Ops:
  7.2 0.0 all-gather.10.cloned.1.call-start
  7.2 0.7 all-gather.10.cloned.1.call-update
  7.9 14.4 %all_to_all.28 = bf16[32,16,8016]{2,1,0:T(8,128)(2,1)} reshape(bf16[32,128256]{1,0:T(8,128)(2,1)} %param.3) | data formatting | bytes 16416768 | tf_op jit(solution)/shard_map/all_to_all | solution.py:47
  22.3 8.0 %copy.10 = bf16[32,16,8016]{2,0,1:T(8,128)(2,1)} copy(bf16[32,16,8016]{2,1,0:T(8,128)(2,1)} %all_to_all.28) | data formatting | bytes 16416768 | tf_op jit(solution)/shard_map/all_to_all | solution.py:47
  30.3 129.8 %all_to_all.38 = bf16[32,16,8016]{2,0,1:T(8,128)(2,1)} all-to-all(bf16[32,16,8016]{2,0,1:T(8,128)(2,1)} %copy.10), channel_id=1, replica_groups=mesh['dp_0'=4,'dp_1'=2,'tp_0'=4,'tp_1'=4] {'tp_0','tp_1'}, dimensions={1} | all-to-all | bytes 16416768 | tf_op jit(solution)/shard_map/all_to_all | solution.py:47
  160.1 18.6 %all_to_all.32 = bf16[512,8,1002]{2,1,0:T(8,128)(2,1)} reshape(bf16[16,32,8016]{2,1,0:T(8,128)(2,1)} %bitcast.203) | data formatting | bytes 16416768 | tf_op jit(solution)/shard_map/all_to_all | solution.py:48
  178.7 12.5 %copy.11 = bf16[512,8,1002]{0,2,1:T(8,128)(2,1)} copy(bf16[512,8,1002]{2,1,0:T(8,128)(2,1)} %all_to_all.32) | data formatting | bytes 16416768 | tf_op jit(solution)/shard_map/all_to_all | solution.py:48
  191.2 5.4 %all-to-all-start.1 = ((bf16[512,8,1002]{0,2,1:T(8,128)(2,1)}), bf16[512,8,1002]{0,2,1:T(8,128)(2,1)}, u32[]{:S(2)}, u32[]{:S(2)}) async-start(bf16[512,8,1002]{0,2,1:T(8,128)(2,1)} %copy.11), calls=%async_computation.1 | async-start | bytes 16515072 | tf_op jit(solution)/shard_map/all_to_all | solution.py:48
  196.6 0.0 copy-done
  196.6 0.3 dynamic-update-slice
  196.9 146.1 %all-reduce = s32[2048]{0:T(1024)S(1)} all-reduce(s32[2048]{0:T(1024)S(1)} %dynamic-update-slice), channel_id=1, replica_groups=mesh['dp_0'=4,'dp_1'=2,'tp_0'=4,'tp_1'=4] {'dp_0','dp_1','tp_0','tp_1'}, use_global_device_ids=true, to_apply=%add | all-reduce | flops 2048 | bytes 16384
  342.9 11.7 %copy.13 = bf16[512,8016]{0,1:T(8,128)(2,1)} copy(bf16[512,8016]{1,0:T(8,128)(2,1)} %bitcast.204) | data formatting | bytes 16416768
  354.6 0.0 all-to-all-done.1
  354.6 12.1 %copy.12 = bf16[8,512,1002]{2,1,0:T(8,128)(2,1)} copy(bf16[8,512,1002]{1,2,0:T(8,128)(2,1)} %bitcast.2) | data formatting | bytes 16416768 | tf_op jit(solution)/shard_map/all_to_all | solution.py:48
  366.8 22.6 %fusion.41 = (f32[2048]{0:T(1024)S(1)}, f32[2048,1002]{0,1:T(8,128)S(1)}) fusion(bf16[2048,4096]{1,0:T(8,128)(2,1)} %all-gather.10.cloned.1.call-done, bf16[4096,1002]{1,0:T(8,128)(2,1)} %bitcast.205), kind=kOutput, calls=%fused_computation.81 | convolution fusion | flops 16812820480 | bytes 33202176 | tf_op jit(solution)/shard_map/dot_general | solution.py:54
  389.4 2.3 exponential_reduce_fusion
  391.7 12.0 %all-gather.4 = f32[4,3,2048]{2,1,0:T(4,128)S(1)} all-gather(f32[1,3,2048]{2,1,0:T(4,128)S(1)} %maximum_bitcast_fusion), channel_id=2, replica_groups=mesh['dp_0'=4,'dp_1'=2,'tp_0'=4,'tp_1'=4] {'dp_0'}, dimensions={0}, use_global_device_ids=true | all-gather | bytes 122880 | tf_op jit(solution)/shard_map/all_gather | solution.py:20
  403.8 0.1 fusion.16
  403.9 1.9 all-gather.5
  405.8 12.0 %all-gather.6 = f32[4,3,2048]{2,1,0:T(4,128)S(1)} all-gather(f32[1,3,2048]{2,1,0:T(4,128)S(1)} %maximum_bitcast_fusion.2), channel_id=4, replica_groups=mesh['dp_0'=4,'dp_1'=2,'tp_0'=4,'tp_1'=4] {'tp_0'}, dimensions={0}, use_global_device_ids=true | all-gather | bytes 122880 | tf_op jit(solution)/shard_map/all_gather | solution.py:20
  417.9 0.1 fusion.2
  418.0 12.0 %all-gather.7 = f32[4,3,2048]{2,1,0:T(4,128)S(1)} all-gather(f32[1,3,2048]{2,1,0:T(4,128)S(1)} %maximum_bitcast_fusion.3), channel_id=5, replica_groups=mesh['dp_0'=4,'dp_1'=2,'tp_0'=4,'tp_1'=4] {'tp_1'}, dimensions={0}, use_global_device_ids=true | all-gather | bytes 122880 | tf_op jit(solution)/shard_map/all_gather | solution.py:20
  430.0 0.1 fusion.40
  430.1 0.6 dynamic-slice_subtract_fusion
  (13 shorter events, 0.3 us)
Async XLA Ops:
  7.2 359.6 %all-gather.10.cloned.1.call-start = ((), (), s32[]{:S(2)}) async-start(), calls=%async_computation.2 | async-start | bytes 16908288 | tf_op jit(solution)/shard_map/all_gather | solution.py:51
  191.2 5.4 %copy-start = (s32[16]{0:T(128)S(1)}, s32[16]{0:T(128)}, u32[]{:S(2)}) copy-start(s32[16]{0:T(128)} %param.5) | copy-start | bytes 196
  191.2 163.5 %all-to-all-start.1 = ((bf16[512,8,1002]{0,2,1:T(8,128)(2,1)}), bf16[512,8,1002]{0,2,1:T(8,128)(2,1)}, u32[]{:S(2)}, u32[]{:S(2)}) async-start(bf16[512,8,1002]{0,2,1:T(8,128)(2,1)} %copy.11), calls=%async_computation.1 | async-start | bytes 16515072 | tf_op jit(solution)/shard_map/all_to_all | solution.py:48
Sparse Core Ops, SparseCore 0:
  11.1 148.0 all-gather.9
where the time goes:
time: 439 us; the launch traced here: 438 us
  blocking collectives  314 us (72%)
  local copies, waits for them, and re-layouts  77.6 us (18%)
  matrix products  22.6 us (5%)
  between operations  14.1 us (3%)
  starting transfers between devices  5.43 us (1%)
    unnamed x1, blocking collectives  146 us
    all_to_all x1, blocking collectives, shards(): lax.all_to_all(head_fsdp, TP, split_axis=1, concat_axis=0, tiled=True)  130 us
    all_to_all x3, local copies, waits for them, and re-layouts, shards(): lax.all_to_all(head_tp, DP, split_axis=1, concat_axis=0, tiled=True)  43.2 us
    all_gather x4, blocking collectives, all_in_one(): both, at, found = (lax.all_gather(jnp.concatenate(lines), axis), 0, {})  37.8 us
    dot_general x1, matrix products, shards(): logits = jnp.dot(all_hidden, head_full, preferred_element_type=jnp.float32)  22.6 us
    all_to_all x2, local copies, waits for them, and re-layouts, shards(): lax.all_to_all(head_fsdp, TP, split_axis=1, concat_axis=0, tiled=True)  22.4 us
    unnamed x5, local copies, waits for them, and re-layouts  12 us
  transfers between devices with their start and end apart: 2, of which 0 were waited for; matrix products, arithmetic and copies ran while one was open for 10% of the time, Pallas kernels for 0%

commit v1 on v0

--- a/solution.py
+++ b/solution.py
@@ -44,7 +44,9 @@
 
 
 def shards(head_fsdp, hidden, targets):
-    head_tp = lax.all_to_all(head_fsdp, TP, split_axis=1, concat_axis=0, tiled=True)
+    head_tp = jnp.concatenate(
+        lax.all_to_all(jnp.stack(jnp.split(head_fsdp, lax.axis_size(TP), axis=1)), TP, 0, 0), axis=0
+    )
     head_full = lax.all_to_all(head_tp, DP, split_axis=1, concat_axis=0, tiled=True)
     vocab_start = lax.axis_index(TP) * head_tp.shape[1] + lax.axis_index(DP) * head_full.shape[1]
     all_hidden, all_targets = (

time: 439 us -> 413 us (0.941)
  blocking collectives: 314 us -> 296 us
  local copies, waits for them, and re-layouts: 77.6 us -> 67.3 us
    all_to_all x2 -> x0, local copies, waits for them, and re-layouts: 22.4 us -> none  [shards(): lax.all_to_all(head_fsdp, TP, split_axis=1, concat_axis=0, tiled=True)]
    all_to_all x1, blocking collectives: 130 us -> 113 us  [shards(): lax.all_to_all(jnp.stack(jnp.split(head_fsdp, lax.axis_size(TP), axis=1))...]
    unnamed x5 -> x22, local copies, waits for them, and re-layouts: 12 us -> 23.6 us
  transfers between devices with their start and end apart: 2 -> 2, of which waited for: 0 -> 0; matrix products, arithmetic and copies ran while one was open for 10% -> 12% of each run, Pallas kernels for 0% -> 0%
where the time goes in v1:
time: 413 us; the launch traced here: 411 us
  blocking collectives  296 us (72%)
  local copies, waits for them, and re-layouts  67.3 us (16%)
  matrix products  22.9 us (6%)
  between operations  14.2 us (3%)
  starting transfers between devices  6.02 us (1%)
    unnamed x1, blocking collectives  146 us
    all_to_all x1, blocking collectives, shards(): lax.all_to_all(jnp.stack(jnp.split(head_fsdp, lax.axis_size(TP), axis=1))...  113 us
    all_to_all x3, local copies, waits for them, and re-layouts, shards(): lax.all_to_all(head_tp, DP, split_axis=1, concat_axis=0, tiled=True)  43.5 us
    all_gather x4, blocking collectives, all_in_one(): both, at, found = (lax.all_gather(jnp.concatenate(lines), axis), 0, {})  37.8 us
    unnamed x22, local copies, waits for them, and re-layouts  23.6 us
    dot_general x1, matrix products, shards(): logits = jnp.dot(all_hidden, head_full, preferred_element_type=jnp.float32)  22.9 us
  transfers between devices with their start and end apart: 2, of which 0 were waited for; matrix products, arithmetic and copies ran while one was open for 12% of the time, Pallas kernels for 0%

profile of v1, /device:TPU:0, one launch (start us, length us, event | category | flops | bytes accessed | tf_op | source)
XLA Modules:
  0.0 410.9 jit_solution(10634856548962990820)
XLA Ops:
  7.2 0.7 all-gather.10.cloned.1.call-update
  7.9 1.2 bitcast_dynamic-update-slice_fusion.15
  9.1 1.5 bitcast_dynamic-update-slice_fusion.14
  10.6 1.3 bitcast_dynamic-update-slice_fusion.13
  11.9 1.3 bitcast_dynamic-update-slice_fusion.12
  13.1 1.3 bitcast_dynamic-update-slice_fusion.11
  14.4 1.3 bitcast_dynamic-update-slice_fusion.10
  15.6 1.3 bitcast_dynamic-update-slice_fusion.9
  16.9 1.3 bitcast_dynamic-update-slice_fusion.8
  19.7 112.8 %all_to_all.24 = bf16[16,32,8016]{2,1,0:T(8,128)(2,1)} all-to-all(bf16[16,32,8016]{2,1,0:T(8,128)(2,1)S(1)} %bitcast_dynamic-update-slice_fusion), channel_id=1, replica_groups=mesh['dp_0'=4,'dp_1'=2,'tp_0'=4,'tp_1'=4] {'tp_0','tp_1'}, dimensions={0} | all-to-all | bytes 16416768 | tf_op jit(solution)/shard_map/all_to_all | solution.py:48
  132.5 18.9 %all_to_all.18 = bf16[512,8,1002]{2,1,0:T(8,128)(2,1)} reshape(bf16[16,32,8016]{2,1,0:T(8,128)(2,1)} %all_to_all.24) | data formatting | bytes 16416768 | tf_op jit(solution)/shard_map/all_to_all | solution.py:50
  151.4 12.5 %copy.9 = bf16[512,8,1002]{0,2,1:T(8,128)(2,1)} copy(bf16[512,8,1002]{2,1,0:T(8,128)(2,1)} %all_to_all.18) | data formatting | bytes 16416768 | tf_op jit(solution)/shard_map/all_to_all | solution.py:50
  163.9 6.0 %all-to-all-start.1 = ((bf16[512,8,1002]{0,2,1:T(8,128)(2,1)}), bf16[512,8,1002]{0,2,1:T(8,128)(2,1)}, u32[]{:S(2)}, u32[]{:S(2)}) async-start(bf16[512,8,1002]{0,2,1:T(8,128)(2,1)} %copy.9), calls=%async_computation.1 | async-start | bytes 16515072 | tf_op jit(solution)/shard_map/all_to_all | solution.py:50
  169.9 0.3 dynamic-update-slice
  170.2 145.8 %all-reduce = s32[2048]{0:T(1024)S(1)} all-reduce(s32[2048]{0:T(1024)S(1)} %dynamic-update-slice), channel_id=1, replica_groups=mesh['dp_0'=4,'dp_1'=2,'tp_0'=4,'tp_1'=4] {'dp_0','dp_1','tp_0','tp_1'}, use_global_device_ids=true, to_apply=%add | all-reduce | flops 2048 | bytes 16384
  316.0 11.7 %copy.11 = bf16[512,8016]{0,1:T(8,128)(2,1)} copy(bf16[512,8016]{1,0:T(8,128)(2,1)} %bitcast.242) | data formatting | bytes 16416768
  327.7 12.2 %copy.10 = bf16[8,512,1002]{2,1,0:T(8,128)(2,1)} copy(bf16[8,512,1002]{1,2,0:T(8,128)(2,1)} %bitcast.17) | data formatting | bytes 16416768 | tf_op jit(solution)/shard_map/all_to_all | solution.py:50
  339.9 22.9 %fusion.44 = (f32[2048]{0:T(1024)S(1)}, f32[1002,2048]{1,0:T(8,128)S(1)}) fusion(bf16[4096,1002]{1,0:T(8,128)(2,1)} %bitcast.243, bf16[2048,4096]{1,0:T(8,128)(2,1)} %all-gather.10.cloned.1.call-done), kind=kOutput, calls=%fused_computation.100 | convolution fusion | flops 16812820480 | bytes 33202176 | tf_op jit(solution)/shard_map/dot_general | solution.py:56
  362.8 2.3 fusion.1
  365.1 12.0 %all-gather.4 = f32[4,3,2048]{2,1,0:T(4,128)S(1)} all-gather(f32[1,3,2048]{2,1,0:T(4,128)S(1)} %maximum_bitcast_fusion), channel_id=2, replica_groups=mesh['dp_0'=4,'dp_1'=2,'tp_0'=4,'tp_1'=4] {'dp_0'}, dimensions={0}, use_global_device_ids=true | all-gather | bytes 122880 | tf_op jit(solution)/shard_map/all_gather | solution.py:20
  377.3 1.9 all-gather.5
  379.2 12.0 %all-gather.6 = f32[4,3,2048]{2,1,0:T(4,128)S(1)} all-gather(f32[1,3,2048]{2,1,0:T(4,128)S(1)} %maximum_bitcast_fusion.2), channel_id=4, replica_groups=mesh['dp_0'=4,'dp_1'=2,'tp_0'=4,'tp_1'=4] {'tp_0'}, dimensions={0}, use_global_device_ids=true | all-gather | bytes 122880 | tf_op jit(solution)/shard_map/all_gather | solution.py:20
  391.4 12.0 %all-gather.7 = f32[4,3,2048]{2,1,0:T(4,128)S(1)} all-gather(f32[1,3,2048]{2,1,0:T(4,128)S(1)} %maximum_bitcast_fusion.3), channel_id=5, replica_groups=mesh['dp_0'=4,'dp_1'=2,'tp_0'=4,'tp_1'=4] {'tp_1'}, dimensions={0}, use_global_device_ids=true | all-gather | bytes 122880 | tf_op jit(solution)/shard_map/all_gather | solution.py:20
  403.5 0.6 dynamic-slice_subtract_fusion
  (29 shorter events, 2.1 us)
Async XLA Ops:
  7.2 332.7 %all-gather.10.cloned.1.call-start = ((), (), s32[]{:S(2)}) async-start(), calls=%async_computation.2 | async-start | bytes 16908288 | tf_op jit(solution)/shard_map/all_gather | solution.py:53
  7.9 10.3 %copy-start = (bf16[32,128256]{1,0:T(8,128)(2,1)S(1)}, bf16[32,128256]{1,0:T(8,128)(2,1)}, u32[]{:S(2)}) copy-start(bf16[32,128256]{1,0:T(8,128)(2,1)} %param.3) | copy-start | bytes 24625156
  163.9 6.0 %copy-start.1 = (s32[16]{0:T(128)S(1)}, s32[16]{0:T(128)}, u32[]{:S(2)}) copy-start(s32[16]{0:T(128)} %param.5) | copy-start | bytes 196
  163.9 163.8 %all-to-all-start.1 = ((bf16[512,8,1002]{0,2,1:T(8,128)(2,1)}), bf16[512,8,1002]{0,2,1:T(8,128)(2,1)}, u32[]{:S(2)}, u32[]{:S(2)}) async-start(bf16[512,8,1002]{0,2,1:T(8,128)(2,1)} %copy.9), calls=%async_computation.1 | async-start | bytes 16515072 | tf_op jit(solution)/shard_map/all_to_all | solution.py:50
Sparse Core Ops, SparseCore 0:
  11.1 138.4 all-gather.9
